TPU v7x, 32 devices: a whole 2x2x4 slice. The times are simulated.
32 devices in a mesh: tm: 8 (over y, x, core), space: 4 (over z).
Axes of the slice: x: 2, y: 2, z: 4, core: 2. Of those that a mesh axis runs over, the one named last changes fastest.
Arguments:
- initial_density: float32 [96, 512], P('space'), may hold values from 0.5 to 2
- terminal_cost: float32 [96, 512], P('space'), may hold values from -1.2 to 1.2
- running_cost: float32 [96, 512], P('space'), may hold values from -0.3 to 0.3
- discount_rate: float32 [96, 512], P('space'), may hold values from 0.003 to 0.5
- slice_steps: int32 [8], replicated, may hold values from 4 to 8
Outputs:
- density_path: float32 [8, 96, 512], P('tm', 'space')
- value_path: float32 [8, 96, 512], P('tm', 'space')
All inputs are finite; a program needn't handle non-finite values.
Results may differ from a plain program's by a relative error of at most 0.0003.
Values sent between devices are 32-bit elements; how exact they have to be, the bound alone decides.
A program may use at most 64 MiB of HBM per device.

v0:
```python
import jax
import jax.numpy as jnp
from jax import lax
from jax.sharding import PartitionSpec as P

K = 8
ITERS = 2


time_step = 0.05
diffusion = 2.0
coupling = 0.1


def extended(block, sides, width):
    for axis, dim in sides:
        count = lax.axis_size(axis)
        forward = [(i, i + 1) for i in range(count - 1)]
        forward.append((count - 1, 0))
        backward = [(target, source) for source, target in forward]
        low = lax.ppermute(
            lax.slice_in_dim(block, block.shape[dim] - width, None, axis=dim), axis, forward
        )
        high = lax.ppermute(lax.slice_in_dim(block, 0, width, axis=dim), axis, backward)
        block = jnp.concatenate([low, block, high], axis=dim)
    return block


def prefix(value, axis, join, neutral, backward):
    count, mine = (lax.axis_size(axis), lax.axis_index(axis))
    pieces = jax.tree.map(lambda part: lax.all_gather(part, axis), value)
    if backward:
        pieces = jax.tree.map(lambda part: part[::-1], pieces)
        mine = count - 1 - mine
    running = jax.tree.map(
        lambda part, zero: jnp.full_like(part, 0) + jnp.asarray(zero, part.dtype), value, neutral
    )

    def lap(position, running):
        longer = join(running, jax.tree.map(lambda part: part[position], pieces))
        return jax.tree.map(lambda new, old: jnp.where(position < mine, new, old), longer, running)

    return lax.fori_loop(0, count - 1, lap, running)


def laplace(padded):
    middle = padded[1:-1]
    return (
        padded[2:] + padded[:-2] + jnp.roll(middle, 1, 1) + jnp.roll(middle, -1, 1) - 4.0 * middle
    )


def slopes(padded):
    middle = padded[1:-1]
    return (
        0.5 * (padded[2:] - padded[:-2]),
        0.5 * (jnp.roll(middle, -1, 1) - jnp.roll(middle, 1, 1)),
    )


def value_step(padded, source):
    slope_across, slope_along = slopes(padded)
    hamilton = 0.5 * (slope_across * slope_across + slope_along * slope_along)
    return padded[1:-1] + time_step * (diffusion * laplace(padded) - hamilton + source)


def density_step(density, value):
    slope_across, slope_along = slopes(value)
    flux_across = density * slope_across
    flux_along = density * slope_along
    inner = flux_along[1:-1]
    divergence = 0.5 * (flux_across[2:] - flux_across[:-2]) + 0.5 * (
        jnp.roll(inner, -1, 1) - jnp.roll(inner, 1, 1)
    )
    return density[1:-1] + time_step * (diffusion * laplace(density) + divergence)


def trim_rows(field, width):
    return field[width : field.shape[0] - width]


def fine_deep(density_start, value_end, running_cost, own_steps):
    reach = 2 * K + 1
    padded = extended(jnp.stack([value_end, density_start, running_cost]), (("space", 1),), reach)
    source = padded[2] + coupling * padded[1]
    value_now = padded[0]
    stored = [value_now]
    for substep in range(K):
        active = substep >= K - own_steps
        value_now = jnp.where(
            active, value_step(value_now, trim_rows(source, substep + 1)), trim_rows(value_now, 1)
        )
        stored.append(value_now)
    density_now = trim_rows(padded[1], reach - K)
    for substep in range(K):
        active = substep < own_steps
        density_now = jnp.where(
            active,
            density_step(density_now, trim_rows(stored[K - substep], 2 * substep)),
            trim_rows(density_now, 1),
        )
    return (density_now, trim_rows(value_now, K + 1))


def compose(earlier, latter):
    return (latter[0] * earlier[0], latter[0] * earlier[1] + latter[1])


def on_device(initial_density, terminal_cost, running_cost, discount_rate, slice_steps):
    own_index = lax.axis_index("tm")
    indices = jnp.arange(slice_steps.shape[0], dtype=jnp.int32)
    own_steps = jnp.sum(jnp.where(indices == own_index, slice_steps, 0))
    duration = time_step * own_steps.astype(jnp.float32)
    damping = jnp.exp(-discount_rate * duration)
    ones_field = jnp.ones_like(damping)
    zeros_field = jnp.zeros_like(damping)
    relief = -jnp.expm1(-discount_rate * duration) / discount_rate * running_cost
    factors, offsets = prefix(
        (damping, zeros_field), "tm", compose, (ones_field, zeros_field), False
    )
    density_now = factors * initial_density + offsets
    factors, offsets = prefix((damping, relief), "tm", compose, (ones_field, zeros_field), True)
    value_now = factors * terminal_cost + offsets
    for iteration in range(ITERS):
        fine_density, fine_value = fine_deep(density_now, value_now, running_cost, own_steps)
        density_terms = fine_density - damping * density_now
        value_terms = fine_value - damping * value_now
        factors, offsets = prefix(
            (damping, density_terms), "tm", compose, (ones_field, zeros_field), False
        )
        density_now = factors * initial_density + offsets
        factors, offsets = prefix(
            (damping, value_terms), "tm", compose, (ones_field, zeros_field), True
        )
        value_now = factors * terminal_cost + offsets
    return (density_now[None], value_now[None])


def solution(mesh):
    return jax.shard_map(
        on_device,
        mesh=mesh,
        in_specs=(P("space", None), P("space", None), P("space", None), P("space", None), P()),
        out_specs=(P("tm", "space", None), P("tm", "space", None)),
        check_vma=False,
    )
```

profile of v0, /device:TPU:0, one launch (start us, length us, event | category | flops | bytes accessed | tf_op | source)
XLA Modules:
  0.0 102.6 jit_solution(17766284938196008382)
XLA Ops:
  0.7 0.6 copy-done.3
  1.3 0.7 fusion.250
  2.7 0.9 divide_multiply_fusion
  3.6 11.1 %all-gather = f32[192,512]{1,0:T(8,128)S(1)} all-gather(f32[24,512]{1,0:T(8,128)S(1)} %get-tuple-element.1168), channel_id=2, replica_groups=mesh['tm'=8,'space'=4] {'tm'}, dimensions={0}, use_global_device_ids=true | all-gather | bytes 442368 | tf_op jit(solution)/shard_map/all_gather | solution.py:31
  14.7 9.6 %all-gather.1 = f32[192,512]{1,0:T(8,128)S(1)} all-gather(f32[24,512]{1,0:T(8,128)S(1)} %get-tuple-element.1167), channel_id=3, replica_groups=mesh['tm'=8,'space'=4] {'tm'}, dimensions={0}, use_global_device_ids=true | all-gather | bytes 442368 | tf_op jit(solution)/shard_map/all_gather | solution.py:31
  24.3 0.4 while.96
  24.7 0.4 while.97
  25.1 0.4 copy-done.1
  25.5 0.8 copy-done
  26.3 1.6 %collective-permute-start = (f32[3,17,512]{2,1,0:T(8,128)S(1)}, f32[3,17,512]{2,1,0:T(8,128)S(1)}, u32[]{:S(2)}, u32[]{:S(2)}) collective-permute-start(f32[3,17,512]{2,1,0:T(8,128)S(1)} %get-tuple-element.909), channel_id=1, source_target_pairs={{0,1},{1,2},{2,3},{3,0},{4,5},{5,6},{6,7},{7,4},{8,9},{9,10},{10,1... | collective-permute-start | bytes 313352 | tf_op jit(solution)/shard_map/ppermute | solution.py:21
  28.0 2.2 %collective-permute-start.1 = (f32[3,17,512]{2,1,0:T(8,128)S(1)}, f32[3,17,512]{2,1,0:T(8,128)S(1)}, u32[]{:S(2)}, u32[]{:S(2)}) collective-permute-start(f32[3,17,512]{2,1,0:T(8,128)S(1)} %get-tuple-element.910), channel_id=1, source_target_pairs={{1,0},{2,1},{3,2},{0,3},{5,4},{6,5},{7,6},{4,7},{9,8},{10,9},{11,1... | collective-permute-start | bytes 313352 | tf_op jit(solution)/shard_map/ppermute | solution.py:24
  36.5 0.4 collective-permute-done.1
  37.2 0.1 add_select_fusion.7
  37.4 0.1 fusion.288
  37.5 0.1 add_select_fusion.6
  37.9 0.1 add_select_fusion.5
  38.0 0.1 fusion.280
  38.2 0.1 add_select_fusion.4
  38.5 0.1 add_select_fusion.15
  38.8 0.1 add_select_fusion.14
  39.1 0.1 add_select_fusion.13
  39.4 0.1 add_select_fusion.12
  39.8 0.1 fusion.113
  40.4 0.2 fusion.122
  41.1 0.2 fusion.124
  41.8 0.2 fusion.126
  42.5 0.1 fusion.216
  43.2 0.1 fusion.218
  43.8 0.1 fusion.220
  44.5 0.1 fusion.222
  45.0 8.6 %all-gather.2 = f32[192,512]{1,0:T(8,128)S(1)} all-gather(f32[24,512]{1,0:T(8,128)S(1)} %slice_subtract_fusion.33), channel_id=4, replica_groups=mesh['tm'=8,'space'=4] {'tm'}, dimensions={0}, use_global_device_ids=true | all-gather | bytes 442368 | tf_op jit(solution)/shard_map/all_gather | solution.py:31
  53.6 0.4 while.98
  54.0 0.1 fusion.231
  54.1 9.6 %all-gather.3 = f32[192,512]{1,0:T(8,128)S(1)} all-gather(f32[24,512]{1,0:T(8,128)S(1)} %fusion.231), channel_id=5, replica_groups=mesh['tm'=8,'space'=4] {'tm'}, dimensions={0}, use_global_device_ids=true | all-gather | bytes 442368 | tf_op jit(solution)/shard_map/all_gather | solution.py:31
  63.7 0.3 while.99
  64.1 1.2 %collective-permute-start.2 = (f32[3,17,512]{2,1,0:T(8,128)S(1)}, f32[3,17,512]{2,1,0:T(8,128)S(1)}, u32[]{:S(2)}, u32[]{:S(2)}) collective-permute-start(f32[3,17,512]{2,1,0:T(8,128)S(1)} %get-tuple-element.907), channel_id=1, source_target_pairs={{0,1},{1,2},{2,3},{3,0},{4,5},{5,6},{6,7},{7,4},{8,9},{9,10},{10,1... | collective-permute-start | bytes 313352 | tf_op jit(solution)/shard_map/ppermute | solution.py:21
  65.3 2.7 %collective-permute-start.3 = (f32[3,17,512]{2,1,0:T(8,128)S(1)}, f32[3,17,512]{2,1,0:T(8,128)S(1)}, u32[]{:S(2)}, u32[]{:S(2)}) collective-permute-start(f32[3,17,512]{2,1,0:T(8,128)S(1)} %get-tuple-element.908), channel_id=1, source_target_pairs={{1,0},{2,1},{3,2},{0,3},{5,4},{6,5},{7,6},{4,7},{9,8},{10,9},{11,1... | collective-permute-start | bytes 313352 | tf_op jit(solution)/shard_map/ppermute | solution.py:24
  68.0 4.7 %collective-permute-done.2 = f32[3,17,512]{2,1,0:T(8,128)S(1)} collective-permute-done((f32[3,17,512]{2,1,0:T(8,128)S(1)}, f32[3,17,512]{2,1,0:T(8,128)S(1)}, u32[]{:S(2)}, u32[]{:S(2)}) %collective-permute-start.2) | collective-permute-done | bytes 104480 | tf_op jit(solution)/shard_map/ppermute | solution.py:21
  72.7 1.5 %collective-permute-done.3 = f32[3,17,512]{2,1,0:T(8,128)S(1)} collective-permute-done((f32[3,17,512]{2,1,0:T(8,128)S(1)}, f32[3,17,512]{2,1,0:T(8,128)S(1)}, u32[]{:S(2)}, u32[]{:S(2)}) %collective-permute-start.3) | collective-permute-done | bytes 104480 | tf_op jit(solution)/shard_map/ppermute | solution.py:24
  74.5 0.1 add_select_fusion.3
  74.7 0.1 fusion.270
  74.9 0.1 add_select_fusion.2
  75.2 0.1 add_select_fusion.1
  75.3 0.1 fusion.262
  75.5 0.1 add_select_fusion
  75.8 0.1 add_select_fusion.11
  76.2 0.1 add_select_fusion.10
  76.5 0.1 add_select_fusion.9
  76.8 0.1 add_select_fusion.8
  77.1 0.1 fusion.80
  77.7 0.2 fusion.130
  78.4 0.2 fusion.132
  79.1 0.2 fusion.134
  79.8 0.1 fusion.224
  80.5 0.1 fusion.226
  81.2 0.1 fusion.228
  81.8 0.1 fusion.230
  82.3 8.6 %all-gather.5 = f32[192,512]{1,0:T(8,128)S(1)} all-gather(f32[24,512]{1,0:T(8,128)S(1)} %slice_subtract_fusion.30), channel_id=7, replica_groups=mesh['tm'=8,'space'=4] {'tm'}, dimensions={0}, use_global_device_ids=true | all-gather | bytes 442368 | tf_op jit(solution)/shard_map/all_gather | solution.py:31
  90.9 0.4 while.101
  91.3 0.1 fusion.232
  91.4 9.6 %all-gather.4 = f32[192,512]{1,0:T(8,128)S(1)} all-gather(f32[24,512]{1,0:T(8,128)S(1)} %fusion.232), channel_id=6, replica_groups=mesh['tm'=8,'space'=4] {'tm'}, dimensions={0}, use_global_device_ids=true | all-gather | bytes 442368 | tf_op jit(solution)/shard_map/all_gather | solution.py:31
  101.0 0.3 while.100
  101.3 0.6 add_bitcast_fusion
  102.0 0.6 add_bitcast_fusion.1
  (219 shorter events, 11.8 us)
Async XLA Ops:
  0.7 0.7 copy-start.3
  24.7 0.8 copy-start.1
  24.7 0.8 copy-start.2
  25.5 0.8 copy-start
  26.3 10.2 %collective-permute-start = (f32[3,17,512]{2,1,0:T(8,128)S(1)}, f32[3,17,512]{2,1,0:T(8,128)S(1)}, u32[]{:S(2)}, u32[]{:S(2)}) collective-permute-start(f32[3,17,512]{2,1,0:T(8,128)S(1)} %get-tuple-element.909), channel_id=1, source_target_pairs={{0,1},{1,2},{2,3},{3,0},{4,5},{5,6},{6,7},{7,4},{8,9},{9,10},{10,1... | collective-permute-start | bytes 313352 | tf_op jit(solution)/shard_map/ppermute | solution.py:21
  28.0 9.0 %collective-permute-start.1 = (f32[3,17,512]{2,1,0:T(8,128)S(1)}, f32[3,17,512]{2,1,0:T(8,128)S(1)}, u32[]{:S(2)}, u32[]{:S(2)}) collective-permute-start(f32[3,17,512]{2,1,0:T(8,128)S(1)} %get-tuple-element.910), channel_id=1, source_target_pairs={{1,0},{2,1},{3,2},{0,3},{5,4},{6,5},{7,6},{4,7},{9,8},{10,9},{11,1... | collective-permute-start | bytes 313352 | tf_op jit(solution)/shard_map/ppermute | solution.py:24
  64.1 8.6 %collective-permute-start.2 = (f32[3,17,512]{2,1,0:T(8,128)S(1)}, f32[3,17,512]{2,1,0:T(8,128)S(1)}, u32[]{:S(2)}, u32[]{:S(2)}) collective-permute-start(f32[3,17,512]{2,1,0:T(8,128)S(1)} %get-tuple-element.907), channel_id=1, source_target_pairs={{0,1},{1,2},{2,3},{3,0},{4,5},{5,6},{6,7},{7,4},{8,9},{9,10},{10,1... | collective-permute-start | bytes 313352 | tf_op jit(solution)/shard_map/ppermute | solution.py:21
  65.3 9.0 %collective-permute-start.3 = (f32[3,17,512]{2,1,0:T(8,128)S(1)}, f32[3,17,512]{2,1,0:T(8,128)S(1)}, u32[]{:S(2)}, u32[]{:S(2)}) collective-permute-start(f32[3,17,512]{2,1,0:T(8,128)S(1)} %get-tuple-element.908), channel_id=1, source_target_pairs={{1,0},{2,1},{3,2},{0,3},{5,4},{6,5},{7,6},{4,7},{9,8},{10,9},{11,1... | collective-permute-start | bytes 313352 | tf_op jit(solution)/shard_map/ppermute | solution.py:24
where the time goes:
time: 103 us
  blocking collectives  56.9 us (55%)
  local copies, waits for them, and re-layouts  12.4 us (12%)
  other arithmetic  9.01 us (9%)
  between operations  8.66 us (8%)
  starting transfers between devices  7.75 us (8%)
  waiting for transfers between devices  6.74 us (7%)
  loops' own time  1.13 us (1%)
    all_gather x6, blocking collectives, prefix(): pieces = jax.tree.map(lambda part: lax.all_gather(part, axis), value)  56.9 us
    ppermute x2, starting transfers between devices, extended(): lax.ppermute(lax.slice_in_dim(block, 0, width, axis=dim), axis, backward)  4.94 us
    slice x60, local copies, waits for them, and re-layouts, laplace(): jnp.roll(middle, 1, 1)  4.94 us
    ppermute x2, waiting for transfers between devices, extended(): lax.ppermute(lax.slice_in_dim(block, block.shape[dim] - width, None, axis...  4.74 us
    ppermute x2, starting transfers between devices, extended(): lax.ppermute(lax.slice_in_dim(block, block.shape[dim] - width, None, axis...  2.81 us
    slice x32, local copies, waits for them, and re-layouts, slopes(): jnp.roll(middle, 1, 1)  2.57 us
    slice x28, local copies, waits for them, and re-layouts, density_step(): jnp.roll(inner, -1, 1) - jnp.roll(inner, 1, 1)  2.25 us
    select_n x16, other arithmetic, fine_deep(): jnp.where(active, value_step(value_now, trim_rows(source, substep + 1)),...  2.13 us
  transfers between devices with their start and end apart: 4, of which 3 were waited for; matrix products, arithmetic and copies ran while one was open for 0% of the time, Pallas kernels for 0%

commit v1 on v0

v1 whole, which is shorter than its diff:
```python
import functools

import jax
import jax.numpy as jnp
from jax import lax
from jax.experimental import pallas as pl
from jax.experimental.pallas import tpu as pltpu
from jax.sharding import PartitionSpec as P

K = 8
ITERS = 2
TIME_STEP = 0.05
DIFFUSION = 2.0
COUPLING = 0.1
REACH = 24
MARGIN = 16
INNER = 8
MESH = pl.DeviceIdType.MESH


def shifted(field, dim):
    size = field.shape[dim]
    return pltpu.roll(field, 1, dim), pltpu.roll(field, size - 1, dim)


def rise(field, dim):
    before, after = shifted(field, dim)
    return after - before


def grown(exponent, power):
    series = 1.0 + exponent * (1.0 / 8.0)
    for order in range(7, 1, -1):
        series = 1.0 + exponent * (1.0 / order) * series
    return jnp.where(jnp.abs(exponent) < 0.35, exponent * series, power - 1.0)


def value_step(value, source, dt):
    up, down = shifted(value, 0)
    left, right = shifted(value, 1)
    across, along = down - up, right - left
    k = dt * DIFFUSION
    total = (up + down) + (left + right)
    hamilton = across * across + along * along
    new = value * (1.0 - 4.0 * k) + (k * total + dt * (source - 0.125 * hamilton))
    return new, across, along


def density_step(density, across, along, dt):
    k, kk = dt * DIFFUSION, dt * 0.25
    pa, pb = kk * across, kk * along
    size = density.shape
    return (
        density * (1.0 - 4.0 * k)
        + (pltpu.roll(density * (k + pa), size[0] - 1, 0) + pltpu.roll(density * (k - pa), 1, 0))
        + (pltpu.roll(density * (k + pb), size[1] - 1, 1) + pltpu.roll(density * (k - pb), 1, 1))
    )


def kernel(
    n, ring, steps, m0_in, ut_in, rc_in, rate_in, m_out, u_out,
    raw, path, ubuf, source, slopes, dbuf, damp,
    term, pair, chipsum, gathered,
    load_sem, halo_send, halo_recv, path_send, path_recv,
    pair_send, pair_recv, sum_send, sum_recv,
):
    rows, cols = m0_in.shape
    chips = n // 2
    me, place = lax.axis_index("tm"), lax.axis_index("space")
    chip, core = me // 2, me % 2
    partner = chip * 2 + 1 - core
    above, below = lax.rem(place + ring - 1, ring), lax.rem(place + 1, ring)
    own = pl.ds(rows, rows)
    inputs = (m0_in, ut_in, rc_in, rate_in)

    loads = [
        pltpu.make_async_copy(ref, raw.at[f, own], load_sem.at[f]) for f, ref in enumerate(inputs)
    ]
    for load in loads:
        load.start()

    barrier = pltpu.get_barrier_semaphore()
    pl.semaphore_signal(barrier, inc=1, device_id=(partner, place), device_id_type=MESH)
    for other in (above, below):
        pl.semaphore_signal(barrier, inc=1, device_id=(me, other), device_id_type=MESH)
    for hop in range(1, chips):
        peer = lax.rem(chip + hop, chips) * 2 + core
        pl.semaphore_signal(barrier, inc=1, device_id=(peer, place), device_id_type=MESH)
    pl.semaphore_wait(barrier, 2 + chips)

    def halo(src, dst, send, recv, width):
        return [
            pltpu.make_async_remote_copy(
                src_ref=src.at[pl.ds(rows - width, width)],
                dst_ref=dst.at[pl.ds(rows - width, width)],
                send_sem=send.at[0], recv_sem=recv.at[0],
                device_id=(me, below), device_id_type=MESH,
            ),
            pltpu.make_async_remote_copy(
                src_ref=src.at[pl.ds(0, width)],
                dst_ref=dst.at[pl.ds(2 * rows, width)],
                send_sem=send.at[1], recv_sem=recv.at[1],
                device_id=(me, above), device_id_type=MESH,
            ),
        ]

    first = []
    for f in (3, 1, 2, 0):
        width = MARGIN if f == 0 else REACH
        first += halo(inputs[f], raw.at[f], halo_send.at[f], halo_recv.at[f], width)
    for copy in first:
        copy.start()

    own_steps = steps[me]
    zero = jnp.int32(0)
    before, after = zero, zero
    for j in range(n):
        before = before + jnp.where(j < me, steps[j], 0)
        after = after + jnp.where(j > me, steps[j], 0)

    def lasting(count):
        return TIME_STEP * count.astype(jnp.float32)

    for load in loads:
        load.wait()
    rate_own = raw[3, own]
    for c in range(chips):
        damp[c] = jnp.exp(-rate_own * lasting(steps[2 * c] + steps[2 * c + 1]))
    damp_own = jnp.exp(-rate_own * lasting(own_steps))
    damp_partner = jnp.exp(-rate_own * lasting(steps[partner]))
    damp[chips] = damp_own
    damp[chips + 1] = damp_partner

    for copy in first:
        copy.wait_recv()
    rate = raw[3]
    path[0, 0] = jnp.exp(-rate * lasting(before)) * raw[0]
    gone = -rate * lasting(after)
    kept = jnp.exp(gone)
    path[0, 1] = kept * raw[1] - grown(gone, kept) / rate * raw[2]

    wide = pl.ds(rows - MARGIN, rows + 2 * MARGIN)

    def meet(it, kind):
        return pltpu.make_async_remote_copy(
            src_ref=term.at[it, kind], dst_ref=pair.at[it, kind],
            send_sem=pair_send.at[it, kind], recv_sem=pair_recv.at[it, kind],
            device_id=(partner, place), device_id_type=MESH,
        )

    def spread(it, kind, slot, target):
        return pltpu.make_async_remote_copy(
            src_ref=chipsum.at[it, kind], dst_ref=gathered.at[it, kind, slot],
            send_sem=sum_send.at[it, kind, target], recv_sem=sum_recv.at[it, kind, slot],
            device_id=(target * 2 + core, place), device_id_type=MESH,
        )

    def needs(kind, target):
        return target > chip if kind == 0 else target < chip

    def send_sums(it, kind):
        mine, theirs = term[it, kind], pair[it, kind]
        mine_last = core == (1 if kind == 0 else 0)
        chipsum[it, kind] = jnp.where(
            mine_last, damp[chips] * theirs + mine, damp[chips + 1] * mine + theirs
        )
        for target in range(chips):
            @pl.when(needs(kind, target))
            def _():
                spread(it, kind, chip, target).start()

    def collect(it, kind, into):
        into[...] = raw[kind, own]
        for c in range(chips) if kind == 0 else range(chips - 1, -1, -1):
            @pl.when(c < chip if kind == 0 else c > chip)
            def _():
                spread(it, kind, c, c).wait_recv()
                into[...] = damp[c] * into[...] + gathered[it, kind, c]

        @pl.when(core == (1 if kind == 0 else 0))
        def _():
            into[...] = damp[chips + 1] * into[...] + pair[it, kind]

    for it in range(ITERS):
        last = it == ITERS - 1
        field = raw[2] + COUPLING * path[it, 0]
        source[...] = field[rows - MARGIN : 2 * rows + MARGIN]

        def dt_value(q):
            return jnp.where(q >= K - own_steps, TIME_STEP, 0.0).astype(jnp.float32)

        def dt_density(i):
            return jnp.where(i < own_steps, TIME_STEP, 0.0).astype(jnp.float32)

        new, _, _ = value_step(path[it, 1], field, dt_value(0))
        ubuf[...] = new[rows - MARGIN : 2 * rows + MARGIN]

        cut = slice(MARGIN - INNER, MARGIN + rows + INNER)

        def on_value(q, carry):
            new, across, along = value_step(ubuf[...], source[...], dt_value(q))
            slopes[q - 1, 0] = across[cut]
            slopes[q - 1, 1] = along[cut]
            ubuf[...] = new
            return carry

        lax.fori_loop(1, K, on_value, 0, unroll=K - 1)
        value = ubuf[...]
        term[it, 1] = value[MARGIN : MARGIN + rows] - damp[chips] * path[it, 1, own]
        meet(it, 1).start()
        slopes[K - 1, 0] = rise(value, 0)[cut]
        slopes[K - 1, 1] = rise(value, 1)[cut]

        dbuf[...] = path[it, 0, pl.ds(rows - INNER, rows + 2 * INNER)]

        def on_density(i, carry):
            dbuf[...] = density_step(
                dbuf[...], slopes[K - 1 - i, 0], slopes[K - 1 - i, 1], dt_density(i)
            )
            return carry

        lax.fori_loop(0, K // 2, on_density, 0, unroll=K // 2)
        meet(it, 1).wait_recv()
        send_sums(it, 1)
        lax.fori_loop(K // 2, K, on_density, 0, unroll=K // 2)
        term[it, 0] = dbuf[pl.ds(INNER, rows)] - damp[chips] * path[it, 0, own]
        meet(it, 0).start()

        value_into = u_out.at[0] if last else path.at[it + 1, 1, own]
        collect(it, 1, value_into)
        if not last:
            on_way = halo(value_into, path.at[it + 1, 1], path_send.at[it, 1], path_recv.at[it, 1], REACH)
            for copy in on_way:
                copy.start()
        meet(it, 0).wait_recv()
        send_sums(it, 0)
        density_into = m_out.at[0] if last else path.at[it + 1, 0, own]
        collect(it, 0, density_into)
        if not last:
            more = halo(density_into, path.at[it + 1, 0], path_send.at[it, 0], path_recv.at[it, 0], MARGIN)
            for copy in more:
                copy.start()
            for copy in on_way + more:
                copy.wait()

    for copy in first:
        copy.wait_send()
    for it in range(ITERS):
        for kind in range(2):
            meet(it, kind).wait_send()
            for target in range(chips):
                @pl.when(needs(kind, target))
                def _():
                    spread(it, kind, chip, target).wait_send()


def on_device(n, ring, initial_density, terminal_cost, running_cost, discount_rate, slice_steps):
    rows, cols = initial_density.shape
    chips = n // 2
    f32 = jnp.float32
    tile = jax.ShapeDtypeStruct((1, rows, cols), f32)
    dma = pltpu.SemaphoreType.DMA
    hbm = pl.BlockSpec(memory_space=pl.ANY)
    vmem = pl.BlockSpec(memory_space=pltpu.VMEM)
    density, value = pl.pallas_call(
        functools.partial(kernel, n, ring),
        out_shape=(tile, tile),
        in_specs=[pl.BlockSpec(memory_space=pltpu.SMEM)] + [hbm] * 4,
        out_specs=(vmem, vmem),
        scratch_shapes=[
            pltpu.VMEM((4, 3 * rows, cols), f32),
            pltpu.VMEM((ITERS, 2, 3 * rows, cols), f32),
            pltpu.VMEM((rows + 2 * MARGIN, cols), f32),
            pltpu.VMEM((rows + 2 * MARGIN, cols), f32),
            pltpu.VMEM((K, 2, rows + 2 * INNER, cols), f32),
            pltpu.VMEM((rows + 2 * INNER, cols), f32),
            pltpu.VMEM((chips + 2, rows, cols), f32),
            pltpu.VMEM((ITERS, 2, rows, cols), f32),
            pltpu.VMEM((ITERS, 2, rows, cols), f32),
            pltpu.VMEM((ITERS, 2, rows, cols), f32),
            pltpu.VMEM((ITERS, 2, chips, rows, cols), f32),
            dma((4,)), dma((4, 2)), dma((4, 2)), dma((ITERS, 2, 2)), dma((ITERS, 2, 2)),
            dma((ITERS, 2)), dma((ITERS, 2)), dma((ITERS, 2, chips)), dma((ITERS, 2, chips)),
        ],
        compiler_params=pltpu.CompilerParams(collective_id=0, has_side_effects=True),
    )(slice_steps, initial_density, terminal_cost, running_cost, discount_rate)
    return density, value


def solution(mesh):
    return jax.shard_map(
        functools.partial(on_device, mesh.shape["tm"], mesh.shape["space"]),
        mesh=mesh,
        in_specs=(P("space", None), P("space", None), P("space", None), P("space", None), P()),
        out_specs=(P("tm", "space", None), P("tm", "space", None)),
        check_vma=False,
    )
```

time: 103 us -> 44.2 us (0.43)
  blocking collectives: 56.9 us -> 0 us
  Pallas kernels: 0 us -> 41.3 us
  local copies, waits for them, and re-layouts: 12.4 us -> 2.06 us
  other arithmetic: 9.01 us -> 0 us
  between operations: 8.66 us -> 0.65 us
  starting transfers between devices: 7.75 us -> 0 us
  waiting for transfers between devices: 6.74 us -> 0 us
  loops' own time: 1.13 us -> 0 us
    all_gather x6 -> x0, blocking collectives: 56.9 us -> none  [prefix(): pieces = jax.tree.map(lambda part: lax.all_gather(part, axis), value)]
    pallas_call x0 -> x1, Pallas kernels: none -> 41.3 us  [on_device(): pl.pallas_call(functools.partial(kernel, n, ring), out_shape=(tile, tile)...]
    slice x134 -> x0, local copies, waits for them, and re-layouts: 10.5 us -> none  [the longest x60 4.94 us: laplace(): jnp.roll(middle, 1, 1)]
    ppermute x4 -> x0, starting transfers between devices: 7.75 us -> none  [the longest x2 4.94 us: extended(): lax.ppermute(lax.slice_in_dim(block, 0, width, axis=dim), axis, backward)]
    ppermute x4 -> x0, waiting for transfers between devices: 6.74 us -> none  [the longest x2 4.74 us: extended(): lax.ppermute(lax.slice_in_dim(block, block.shape[dim] - width, None, axis...]
    mul x31 -> x0, other arithmetic: 3.38 us -> none  [the longest x14 2.02 us: density_step(): flux_along = density * slope_along]
    select_n x58 -> x0, other arithmetic: 3.17 us -> none  [the longest x16 2.13 us: fine_deep(): jnp.where(active, value_step(value_now, trim_rows(source, substep + 1)),...]
    broadcast_in_dim x2 -> x0, other arithmetic: 1.26 us -> none  [on_device(): return (density_now[None], value_now[None])]
  transfers between devices with their start and end apart: 4 -> 0, of which waited for: 3 -> 0; matrix products, arithmetic and copies ran while one was open for 0% -> 0% of each run, Pallas kernels for 0% -> 0%
where the time goes in v1:
time: 44.2 us; the launch traced here: 44 us
  Pallas kernels  41.3 us (93%)
  local copies, waits for them, and re-layouts  2.06 us (5%)
  between operations  0.65 us (1%)
    pallas_call x1, Pallas kernels, on_device(): pl.pallas_call(functools.partial(kernel, n, ring), out_shape=(tile, tile)...  41.3 us
    unnamed x4, local copies, waits for them, and re-layouts  2.06 us

profile of v1, /device:TPU:0, one launch (start us, length us, event | category | flops | bytes accessed | tf_op | source)
XLA Modules:
  0.0 44.0 jit_solution(2305158692538086124)
XLA Ops:
  0.6 41.3 %shard_map.68 = (f32[1,24,512]{2,1,0:T(8,128)}, f32[1,24,512]{2,1,0:T(8,128)}) custom-call(s32[8]{0:T(128)} %steps.1, f32[24,512]{1,0:T(8,128)} %m0_in.1, f32[24,512]{1,0:T(8,128)} %ut_in.1, f32[24,512]{1,0:T(8,128)} %rc_in.1, f32[24,512]{1,0:T(8,128)} %rate_in.1), custom_call_target="tpu_custom_call" | custom-call | tf_op jit(solution)/shard_map/pallas_call | solution.py:265
  41.9 0.0 copy-start
  41.9 1.4 %copy.9 = f32[1,24,512]{2,1,0:T(8,128)} copy(f32[1,24,512]{2,1,0:T(8,128)} %get-tuple-element.4) | data formatting | bytes 98304
  43.3 0.0 copy-done
  43.4 0.6 %copy.10 = f32[1,24,512]{2,1,0:T(8,128)} copy(f32[1,24,512]{2,1,0:T(8,128)S(1)} %copy-done) | data formatting | bytes 98304
Async XLA Ops:
  41.9 1.4 %copy-start = (f32[1,24,512]{2,1,0:T(8,128)S(1)}, f32[1,24,512]{2,1,0:T(8,128)}, u32[]{:S(2)}) copy-start(f32[1,24,512]{2,1,0:T(8,128)} %get-tuple-element.5) | copy-start | bytes 147460

commit v2 on v1

v2 whole, which is shorter than its diff:
```python
import functools

import jax
import jax.numpy as jnp
from jax import lax
from jax.experimental import pallas as pl
from jax.experimental.pallas import tpu as pltpu
from jax.sharding import PartitionSpec as P

K = 8
TIME_STEP = 0.05
DIFFUSION = 2.0
COUPLING = 0.1
LANES = 128
MARGIN = 16
INNER = 8
MESH = pl.DeviceIdType.MESH


def shifted(field, dim):
    size = field.shape[dim]
    return pltpu.roll(field, 1, dim), pltpu.roll(field, size - 1, dim)


def rise(field, dim):
    before, after = shifted(field, dim)
    return after - before


def grown(exponent, power):
    series = 1.0 + exponent * (1.0 / 8.0)
    for order in range(7, 1, -1):
        series = 1.0 + exponent * (1.0 / order) * series
    return jnp.where(jnp.abs(exponent) < 0.35, exponent * series, power - 1.0)


def value_step(value, source, dt):
    up, down = shifted(value, 0)
    left, right = shifted(value, 1)
    across, along = down - up, right - left
    k = dt * DIFFUSION
    total = (up + down) + (left + right)
    hamilton = across * across + along * along
    new = value * (1.0 - 4.0 * k) + (k * total + dt * (source - 0.125 * hamilton))
    return new, across, along


def density_step(density, across, along, dt):
    k, kk = dt * DIFFUSION, dt * 0.25
    pa, pb = kk * across, kk * along
    size = density.shape
    return (
        density * (1.0 - 4.0 * k)
        + (pltpu.roll(density * (k + pa), size[0] - 1, 0) + pltpu.roll(density * (k - pa), 1, 0))
        + (pltpu.roll(density * (k + pb), size[1] - 1, 1) + pltpu.roll(density * (k - pb), 1, 1))
    )


def kernel(
    n, ring, blocks, offsets, steps, m0_in, ut_in, rc_in, rate_in, m_out, u_out,
    stage, raw, first, path, ubuf, source, slopes, dbuf, damp, group_damp,
    term, chain, total, gathered, final, landing,
    load_sem, halo_send, halo_recv, relay_send, relay_recv,
    sum_send, sum_recv, out_send, out_recv,
):
    rows, cols = m0_in.shape
    groups = n // blocks
    per = n // groups
    wide = 2 * LANES
    me, place = lax.axis_index("tm"), lax.axis_index("space")
    block, group = me // groups, me % groups
    half = group % 2
    partner = me + 1 - 2 * half
    slot_of = {offset: pl.ds(i * rows, rows) for i, offset in enumerate(offsets)}
    own = slot_of[0]
    base = (offsets.index(0) - 1) * rows
    near = pl.ds(base, 3 * rows)
    far_offsets = [offset for offset in offsets if offset != 0]
    inputs = (m0_in, ut_in, rc_in, rate_in)

    loads = []
    for f, ref in enumerate(inputs):
        for i, step in enumerate((0, 1, blocks - 1)):
            columns = pl.ds(pl.multiple_of(lax.rem(block + step, blocks) * LANES, LANES), LANES)
            loads.append(pltpu.make_async_copy(ref.at[:, columns], stage.at[i, f], load_sem.at[i, f]))
    for load in loads:
        load.start()

    barrier = pltpu.get_barrier_semaphore()
    for hop in range(1, n):
        pl.semaphore_signal(
            barrier, inc=1, device_id=(lax.rem(me + hop, n), place), device_id_type=MESH
        )
    for offset in far_offsets:
        pl.semaphore_signal(
            barrier, inc=1, device_id=(me, lax.rem(place + ring - offset, ring)), device_id_type=MESH
        )

    for load in loads:
        load.wait()
    lane = lax.broadcasted_iota(jnp.int32, (rows, LANES), 1)
    for f in range(4):
        raw[f, own, :LANES] = stage[0, f]
        raw[f, own, LANES:] = jnp.where(lane < LANES // 2, stage[1, f], stage[2, f])
    pl.semaphore_wait(barrier, n - 1 + len(far_offsets))

    mine = pl.ds(2 * half, 2)
    other = pl.ds(2 - 2 * half, 2)

    def fetch(i, offset):
        return pltpu.make_async_remote_copy(
            src_ref=raw.at[mine, own], dst_ref=raw.at[mine, slot_of[offset]],
            send_sem=halo_send.at[i], recv_sem=halo_recv.at[i],
            device_id=(me, lax.rem(place + ring - offset, ring)), device_id_type=MESH,
        )

    def relay(i, offset, fields):
        return pltpu.make_async_remote_copy(
            src_ref=raw.at[fields, slot_of[offset]], dst_ref=raw.at[fields, slot_of[offset]],
            send_sem=relay_send.at[i], recv_sem=relay_recv.at[i],
            device_id=(partner, place), device_id_type=MESH,
        )

    for i, offset in reversed(list(enumerate(far_offsets))):
        fetch(i, offset).start()

    def lasting(count):
        return TIME_STEP * count.astype(jnp.float32)

    zero = jnp.int32(0)
    for i, offset in enumerate(far_offsets):
        fetch(i, offset).wait_recv()
        relay(i, offset, mine).start()
    for i, offset in enumerate(far_offsets):
        relay(i, offset, other).wait_recv()

    rate = raw[3]
    ratio = raw[2] / rate
    for c in range(groups):
        count = zero
        for j in range(c * per, (c + 1) * per):
            count = count + steps[j]
        group_damp[c] = jnp.exp(-raw[3, near] * lasting(count))
    for i in range(per):
        number = group * per + i
        before, after = zero, zero
        for j in range(n):
            before = before + jnp.where(j < number, steps[j], 0)
            after = after + jnp.where(j > number, steps[j], 0)
        damp[i] = jnp.exp(-raw[3, near] * lasting(steps[number]))
        first[0, i] = jnp.exp(-rate * lasting(before)) * raw[0]
        gone = -rate * lasting(after)
        kept = jnp.exp(gone)
        first[1, i] = kept * raw[1] - grown(gone, kept) * ratio

    def spread(it, kind, slot, target):
        if it == 0:
            src, dst = total.at[kind], gathered.at[kind, slot]
        else:
            src, dst = final.at[0, kind], final.at[1 + slot, kind]
        return pltpu.make_async_remote_copy(
            src_ref=src, dst_ref=dst,
            send_sem=sum_send.at[it, kind, target], recv_sem=sum_recv.at[it, kind, slot],
            device_id=(block * groups + target, place), device_id_type=MESH,
        )

    def needs(kind, target):
        return target > group if kind == 0 else target < group

    def onward(kind, count):
        return range(count) if kind == 0 else range(count - 1, -1, -1)

    def region(it):
        if it == 0:
            return pl.ds(0, 3 * rows), pl.ds(0, wide)
        return pl.ds(rows, rows), pl.ds(0, LANES)

    def send_totals(it, kind):
        r, l = region(it)
        running = None
        for i in onward(kind, per):
            own_term = term[kind, i, r, l]
            running = own_term if running is None else damp[i, r, l] * running + own_term
        if it == 0:
            total[kind] = running
        else:
            final[0, kind] = running
        for target in range(groups):
            @pl.when(needs(kind, target))
            def _():
                spread(it, kind, target=target, slot=group).start()

    def collect(it, kind):
        r, l = region(it)
        start = chain.at[r, l]
        start[...] = raw[kind, near][r.start : r.start + r.size, : l.size]
        for c in onward(kind, groups):
            @pl.when(c < group if kind == 0 else c > group)
            def _():
                spread(it, kind, slot=c, target=c).wait_recv()
                piece = gathered[kind, c] if it == 0 else final[1 + c, kind]
                start[...] = group_damp[c, r, l] * start[...] + piece
        running = start[...]
        order = list(onward(kind, per))
        for i in order:
            if it == 0:
                path[kind, i] = running
            else:
                landed = landing.at[1 + i, kind, :, pl.ds(0, LANES)]
                landed[...] = running
                number = group * per + i

                @pl.when(number != me)
                def _():
                    deliver(kind, i).start()

                @pl.when(number == me)
                def _():
                    landing[0, kind, :, pl.ds(pl.multiple_of(block * LANES, LANES), LANES)] = landed[...]
            if i != order[-1]:
                running = damp[i, r, l] * running + term[kind, i, r, l]

    def deliver(kind, i):
        columns = pl.ds(pl.multiple_of(block * LANES, LANES), LANES)
        return pltpu.make_async_remote_copy(
            src_ref=landing.at[1 + i, kind, :, pl.ds(0, LANES)],
            dst_ref=landing.at[0, kind, :, columns],
            send_sem=out_send.at[kind, i], recv_sem=out_recv.at[kind, block],
            device_id=(group * per + i, place), device_id_type=MESH,
        )

    def arrival(kind, b):
        return pltpu.make_async_remote_copy(
            src_ref=landing.at[1, kind, :, pl.ds(0, LANES)],
            dst_ref=landing.at[0, kind, :, pl.ds(b * LANES, LANES)],
            send_sem=out_send.at[kind, 0], recv_sem=out_recv.at[kind, b],
            device_id=(partner, place), device_id_type=MESH,
        )

    def dt_value(count, q):
        return jnp.where(q >= K - count, TIME_STEP, 0.0).astype(jnp.float32)

    def dt_density(count, i):
        return jnp.where(i < count, TIME_STEP, 0.0).astype(jnp.float32)

    window = raw.shape[1]
    for it in range(2):
        size = window if it == 0 else rows + 2 * MARGIN
        keep = slice(base, base + 3 * rows) if it == 0 else slice(MARGIN - INNER, MARGIN + rows + INNER)
        deep = 3 * rows if it == 0 else rows + 2 * INNER

        def one_value(i, carry):
            count = steps[group * per + i]
            u = ubuf.at[pl.ds(0, size)]
            src = source.at[pl.ds(0, size)]
            if it == 0:
                field = raw[2] + COUPLING * first[0, i]
                src[...] = field
                new, _, _ = value_step(first[1, i], field, dt_value(count, 0))
                u[...] = new
            else:
                field = raw[2, near] + COUPLING * path[0, i]
                inside = slice(rows - MARGIN, 2 * rows + MARGIN)
                src[...] = field[inside]
                new, _, _ = value_step(path[1, i], field, dt_value(count, 0))
                u[...] = new[inside]

            def on_value(q, carry):
                new, across, along = value_step(u[...], src[...], dt_value(count, q))
                slopes[i, q - 1, 0, :deep] = across[keep]
                slopes[i, q - 1, 1, :deep] = along[keep]
                u[...] = new
                return carry

            lax.fori_loop(1, K, on_value, 0, unroll=K - 1)
            value = u[...]
            slopes[i, K - 1, 0, :deep] = rise(value, 0)[keep]
            slopes[i, K - 1, 1, :deep] = rise(value, 1)[keep]
            if it == 0:
                term[1, i] = value[base : base + 3 * rows] - damp[i] * first[1, i, near]
            else:
                r, l = region(it)
                term[1, i, r, l] = value[MARGIN : MARGIN + rows, :LANES] - damp[i, r, l] * path[1, i, r, l]
            return carry

        lax.fori_loop(0, per, one_value, 0)
        send_totals(it, 1)

        def one_density(i, carry):
            count = steps[group * per + i]
            d = dbuf.at[pl.ds(0, deep)]
            d[...] = first[0, i, near] if it == 0 else path[0, i, pl.ds(rows - INNER, deep)]

            def on_density(q, carry):
                d[...] = density_step(
                    d[...], slopes[i, K - 1 - q, 0, :deep], slopes[i, K - 1 - q, 1, :deep],
                    dt_density(count, q),
                )
                return carry

            lax.fori_loop(0, K, on_density, 0, unroll=K)
            if it == 0:
                term[0, i] = d[...] - damp[i] * first[0, i, near]
            else:
                r, l = region(it)
                density = d[...]
                term[0, i, r, l] = density[INNER : INNER + rows, :LANES] - damp[i, r, l] * path[0, i, r, l]
            return carry

        lax.fori_loop(0, per, one_density, 0)
        send_totals(it, 0)
        collect(it, 1)
        collect(it, 0)

    sender = me // per
    for kind, out in ((1, u_out), (0, m_out)):
        for b in range(blocks):
            @pl.when(b * groups + sender != me)
            def _():
                arrival(kind, b).wait_recv()
        out[0] = landing[0, kind]

    for i, offset in enumerate(far_offsets):
        fetch(i, offset).wait_send()
        relay(i, offset, mine).wait_send()
    for kind in range(2):
        for it in range(2):
            for target in range(groups):
                @pl.when(needs(kind, target))
                def _():
                    spread(it, kind, target=target, slot=group).wait_send()
        for i in range(per):
            @pl.when(group * per + i != me)
            def _():
                deliver(kind, i).wait_send()


def on_device(n, ring, initial_density, terminal_cost, running_cost, discount_rate, slice_steps):
    rows, cols = initial_density.shape
    blocks = cols // LANES
    groups = n // blocks
    per = n // groups
    wide = 2 * LANES
    assert groups % 2 == 0 and groups * blocks == n and blocks >= 3 and rows >= 24
    offsets = (-1, 0, 1, 2) if ring == 4 else (-2, -1, 0, 1, 2)
    assert ring >= 4
    window = len(offsets) * rows
    f32 = jnp.float32
    tile = jax.ShapeDtypeStruct((1, rows, cols), f32)
    dma = pltpu.SemaphoreType.DMA
    hbm = pl.BlockSpec(memory_space=pl.ANY)
    vmem = pl.BlockSpec(memory_space=pltpu.VMEM)
    far = len(offsets) - 1
    return pl.pallas_call(
        functools.partial(kernel, n, ring, blocks, offsets),
        out_shape=(tile, tile),
        in_specs=[pl.BlockSpec(memory_space=pltpu.SMEM)] + [hbm] * 4,
        out_specs=(vmem, vmem),
        scratch_shapes=[
            pltpu.VMEM((3, 4, rows, LANES), f32),
            pltpu.VMEM((4, window, wide), f32),
            pltpu.VMEM((2, per, window, wide), f32),
            pltpu.VMEM((2, per, 3 * rows, wide), f32),
            pltpu.VMEM((window, wide), f32),
            pltpu.VMEM((window, wide), f32),
            pltpu.VMEM((per, K, 2, 3 * rows, wide), f32),
            pltpu.VMEM((3 * rows, wide), f32),
            pltpu.VMEM((per, 3 * rows, wide), f32),
            pltpu.VMEM((groups, 3 * rows, wide), f32),
            pltpu.VMEM((2, per, 3 * rows, wide), f32),
            pltpu.VMEM((3 * rows, wide), f32),
            pltpu.VMEM((2, 3 * rows, wide), f32),
            pltpu.VMEM((2, groups, 3 * rows, wide), f32),
            pltpu.VMEM((1 + groups, 2, rows, LANES), f32),
            pltpu.VMEM((1 + per, 2, rows, cols), f32),
            dma((3, 4)), dma((far,)), dma((far,)), dma((far,)), dma((far,)),
            dma((2, 2, groups)), dma((2, 2, groups)), dma((2, per)), dma((2, blocks)),
        ],
        compiler_params=pltpu.CompilerParams(collective_id=0, has_side_effects=True),
    )(slice_steps, initial_density, terminal_cost, running_cost, discount_rate)


def solution(mesh):
    return jax.shard_map(
        functools.partial(on_device, mesh.shape["tm"], mesh.shape["space"]),
        mesh=mesh,
        in_specs=(P("space", None), P("space", None), P("space", None), P("space", None), P()),
        out_specs=(P("tm", "space", None), P("tm", "space", None)),
        check_vma=False,
    )
```

time: 44.2 us -> 34.3 us (0.78)
  Pallas kernels: 41.3 us -> 31.4 us
    pallas_call x1, Pallas kernels: 41.3 us -> 31.4 us  [on_device(): pl.pallas_call(functools.partial(kernel, n, ring, blocks, offsets), out_s...]
where the time goes in v2:
time: 34.3 us; the launch traced here: 34.1 us
  Pallas kernels  31.4 us (92%)
  local copies, waits for them, and re-layouts  2.06 us (6%)
  between operations  0.65 us (2%)
    pallas_call x1, Pallas kernels, on_device(): pl.pallas_call(functools.partial(kernel, n, ring, blocks, offsets), out_s...  31.4 us
    unnamed x4, local copies, waits for them, and re-layouts  2.06 us

profile of v2, /device:TPU:0, one launch (start us, length us, event | category | flops | bytes accessed | tf_op | source)
XLA Modules:
  0.0 34.1 jit_solution(11420948149166476677)
XLA Ops:
  0.6 31.4 %shard_map.68 = (f32[1,24,512]{2,1,0:T(8,128)}, f32[1,24,512]{2,1,0:T(8,128)}) custom-call(s32[8]{0:T(128)} %steps.1, f32[24,512]{1,0:T(8,128)} %m0_in.1, f32[24,512]{1,0:T(8,128)} %ut_in.1, f32[24,512]{1,0:T(8,128)} %rc_in.1, f32[24,512]{1,0:T(8,128)} %rate_in.1), custom_call_target="tpu_custom_call" | custom-call | tf_op jit(solution)/shard_map/pallas_call | solution.py:354
  32.0 0.0 copy-start
  32.0 1.4 %copy.9 = f32[1,24,512]{2,1,0:T(8,128)} copy(f32[1,24,512]{2,1,0:T(8,128)} %get-tuple-element.4) | data formatting | bytes 98304
  33.5 0.0 copy-done
  33.5 0.6 %copy.10 = f32[1,24,512]{2,1,0:T(8,128)} copy(f32[1,24,512]{2,1,0:T(8,128)S(1)} %copy-done) | data formatting | bytes 98304
Async XLA Ops:
  32.0 1.4 %copy-start = (f32[1,24,512]{2,1,0:T(8,128)S(1)}, f32[1,24,512]{2,1,0:T(8,128)}, u32[]{:S(2)}) copy-start(f32[1,24,512]{2,1,0:T(8,128)} %get-tuple-element.5) | copy-start | bytes 147460

commit v3 on v2

--- a/solution.py
+++ b/solution.py
@@ -58,7 +58,7 @@
 
 def kernel(
     n, ring, blocks, offsets, steps, m0_in, ut_in, rc_in, rate_in, m_out, u_out,
-    stage, raw, first, path, ubuf, source, slopes, dbuf, damp, group_damp,
+    stage, raw, parcel, first, path, ubuf, source, slopes, dbuf, damp, group_damp,
     term, chain, total, gathered, final, landing,
     load_sem, halo_send, halo_recv, relay_send, relay_recv,
     sum_send, sum_recv, out_send, out_recv,
@@ -102,21 +102,27 @@
     for f in range(4):
         raw[f, own, :LANES] = stage[0, f]
         raw[f, own, LANES:] = jnp.where(lane < LANES // 2, stage[1, f], stage[2, f])
+
+    central = (lane >= 4 * K) & (lane < LANES - 4 * K)
+    for h in range(2):
+        for k in range(2):
+            parcel[h, k, own] = stage[0, 2 * h + k]
+        parcel[h, 2, own] = jnp.where(
+            central, pltpu.roll(raw[2 * h + 1, own, LANES:], LANES // 2, 1), raw[2 * h, own, LANES:]
+        )
     pl.semaphore_wait(barrier, n - 1 + len(far_offsets))
-
-    mine = pl.ds(2 * half, 2)
-    other = pl.ds(2 - 2 * half, 2)
+    mine, other = half, 1 - half
 
     def fetch(i, offset):
         return pltpu.make_async_remote_copy(
-            src_ref=raw.at[mine, own], dst_ref=raw.at[mine, slot_of[offset]],
+            src_ref=parcel.at[mine, :, own], dst_ref=parcel.at[mine, :, slot_of[offset]],
             send_sem=halo_send.at[i], recv_sem=halo_recv.at[i],
             device_id=(me, lax.rem(place + ring - offset, ring)), device_id_type=MESH,
         )
 
     def relay(i, offset, fields):
         return pltpu.make_async_remote_copy(
-            src_ref=raw.at[fields, slot_of[offset]], dst_ref=raw.at[fields, slot_of[offset]],
+            src_ref=parcel.at[fields, :, slot_of[offset]], dst_ref=parcel.at[fields, :, slot_of[offset]],
             send_sem=relay_send.at[i], recv_sem=relay_recv.at[i],
             device_id=(partner, place), device_id_type=MESH,
         )
@@ -133,6 +139,13 @@
         relay(i, offset, mine).start()
     for i, offset in enumerate(far_offsets):
         relay(i, offset, other).wait_recv()
+    for offset in far_offsets:
+        slot = slot_of[offset]
+        for h in range(2):
+            for k in range(2):
+                raw[2 * h + k, slot, :LANES] = parcel[h, k, slot]
+            raw[2 * h, slot, LANES:] = parcel[h, 2, slot]
+            raw[2 * h + 1, slot, LANES:] = pltpu.roll(parcel[h, 2, slot], LANES // 2, 1)
 
     rate = raw[3]
     ratio = raw[2] / rate
@@ -249,65 +262,62 @@
         keep = slice(base, base + 3 * rows) if it == 0 else slice(MARGIN - INNER, MARGIN + rows + INNER)
         deep = 3 * rows if it == 0 else rows + 2 * INNER
 
-        def one_value(i, carry):
-            count = steps[group * per + i]
-            u = ubuf.at[pl.ds(0, size)]
-            src = source.at[pl.ds(0, size)]
+        counts = [steps[group * per + i] for i in range(per)]
+        u = [ubuf.at[i, pl.ds(0, size)] for i in range(per)]
+        src = [source.at[i, pl.ds(0, size)] for i in range(per)]
+        d = [dbuf.at[i, pl.ds(0, deep)] for i in range(per)]
+        inside = slice(rows - MARGIN, 2 * rows + MARGIN)
+        r, l = region(it)
+
+        for i in range(per):
             if it == 0:
                 field = raw[2] + COUPLING * first[0, i]
-                src[...] = field
-                new, _, _ = value_step(first[1, i], field, dt_value(count, 0))
-                u[...] = new
+                src[i][...] = field
+                new, _, _ = value_step(first[1, i], field, dt_value(counts[i], 0))
+                u[i][...] = new
             else:
                 field = raw[2, near] + COUPLING * path[0, i]
-                inside = slice(rows - MARGIN, 2 * rows + MARGIN)
-                src[...] = field[inside]
-                new, _, _ = value_step(path[1, i], field, dt_value(count, 0))
-                u[...] = new[inside]
-
-            def on_value(q, carry):
-                new, across, along = value_step(u[...], src[...], dt_value(count, q))
+                src[i][...] = field[inside]
+                new, _, _ = value_step(path[1, i], field, dt_value(counts[i], 0))
+                u[i][...] = new[inside]
+
+        def on_value(q, carry):
+            for i in range(per):
+                new, across, along = value_step(u[i][...], src[i][...], dt_value(counts[i], q))
                 slopes[i, q - 1, 0, :deep] = across[keep]
                 slopes[i, q - 1, 1, :deep] = along[keep]
-                u[...] = new
-                return carry
-
-            lax.fori_loop(1, K, on_value, 0, unroll=K - 1)
-            value = u[...]
+                u[i][...] = new
+            return carry
+
+        lax.fori_loop(1, K, on_value, 0)
+        for i in range(per):
+            value = u[i][...]
             slopes[i, K - 1, 0, :deep] = rise(value, 0)[keep]
             slopes[i, K - 1, 1, :deep] = rise(value, 1)[keep]
             if it == 0:
                 term[1, i] = value[base : base + 3 * rows] - damp[i] * first[1, i, near]
             else:
-                r, l = region(it)
                 term[1, i, r, l] = value[MARGIN : MARGIN + rows, :LANES] - damp[i, r, l] * path[1, i, r, l]
+        send_totals(it, 1)
+
+        for i in range(per):
+            d[i][...] = first[0, i, near] if it == 0 else path[0, i, pl.ds(rows - INNER, deep)]
+
+        def on_density(q, carry):
+            for i in range(per):
+                d[i][...] = density_step(
+                    d[i][...], slopes[i, K - 1 - q, 0, :deep], slopes[i, K - 1 - q, 1, :deep],
+                    dt_density(counts[i], q),
+                )
             return carry
 
-        lax.fori_loop(0, per, one_value, 0)
-        send_totals(it, 1)
-
-        def one_density(i, carry):
-            count = steps[group * per + i]
-            d = dbuf.at[pl.ds(0, deep)]
-            d[...] = first[0, i, near] if it == 0 else path[0, i, pl.ds(rows - INNER, deep)]
-
-            def on_density(q, carry):
-                d[...] = density_step(
-                    d[...], slopes[i, K - 1 - q, 0, :deep], slopes[i, K - 1 - q, 1, :deep],
-                    dt_density(count, q),
-                )
-                return carry
-
-            lax.fori_loop(0, K, on_density, 0, unroll=K)
+        lax.fori_loop(0, K, on_density, 0)
+        for i in range(per):
+            density = d[i][...]
             if it == 0:
-                term[0, i] = d[...] - damp[i] * first[0, i, near]
+                term[0, i] = density - damp[i] * first[0, i, near]
             else:
-                r, l = region(it)
-                density = d[...]
                 term[0, i, r, l] = density[INNER : INNER + rows, :LANES] - damp[i, r, l] * path[0, i, r, l]
-            return carry
-
-        lax.fori_loop(0, per, one_density, 0)
         send_totals(it, 0)
         collect(it, 1)
         collect(it, 0)
@@ -359,12 +369,13 @@
         scratch_shapes=[
             pltpu.VMEM((3, 4, rows, LANES), f32),
             pltpu.VMEM((4, window, wide), f32),
+            pltpu.VMEM((2, 3, window, LANES), f32),
             pltpu.VMEM((2, per, window, wide), f32),
             pltpu.VMEM((2, per, 3 * rows, wide), f32),
-            pltpu.VMEM((window, wide), f32),
-            pltpu.VMEM((window, wide), f32),
+            pltpu.VMEM((per, window, wide), f32),
+            pltpu.VMEM((per, window, wide), f32),
             pltpu.VMEM((per, K, 2, 3 * rows, wide), f32),
-            pltpu.VMEM((3 * rows, wide), f32),
+            pltpu.VMEM((per, 3 * rows, wide), f32),
             pltpu.VMEM((per, 3 * rows, wide), f32),
             pltpu.VMEM((groups, 3 * rows, wide), f32),
             pltpu.VMEM((2, per, 3 * rows, wide), f32),

time: 34.3 us -> 28.3 us (0.83)
  Pallas kernels: 31.4 us -> 25.3 us
    pallas_call x1, Pallas kernels: 31.4 us -> 25.3 us  [on_device(): pl.pallas_call(functools.partial(kernel, n, ring, blocks, offsets), out_s...]
where the time goes in v3:
time: 28.3 us; the launch traced here: 28 us
  Pallas kernels  25.3 us (89%)
  local copies, waits for them, and re-layouts  2.06 us (7%)
  between operations  0.65 us (2%)
    pallas_call x1, Pallas kernels, on_device(): pl.pallas_call(functools.partial(kernel, n, ring, blocks, offsets), out_s...  25.3 us
    unnamed x4, local copies, waits for them, and re-layouts  2.06 us

profile of v3, /device:TPU:0, one launch (start us, length us, event | category | flops | bytes accessed | tf_op | source)
XLA Modules:
  0.0 28.0 jit_solution(5085829045131820223)
XLA Ops:
  0.6 25.3 %shard_map.68 = (f32[1,24,512]{2,1,0:T(8,128)}, f32[1,24,512]{2,1,0:T(8,128)}) custom-call(s32[8]{0:T(128)} %steps.1, f32[24,512]{1,0:T(8,128)} %m0_in.1, f32[24,512]{1,0:T(8,128)} %ut_in.1, f32[24,512]{1,0:T(8,128)} %rc_in.1, f32[24,512]{1,0:T(8,128)} %rate_in.1), custom_call_target="tpu_custom_call" | custom-call | tf_op jit(solution)/shard_map/pallas_call | solution.py:364
  26.0 0.0 copy-start
  26.0 1.4 %copy.9 = f32[1,24,512]{2,1,0:T(8,128)} copy(f32[1,24,512]{2,1,0:T(8,128)} %get-tuple-element.4) | data formatting | bytes 98304
  27.4 0.0 copy-done
  27.4 0.6 %copy.10 = f32[1,24,512]{2,1,0:T(8,128)} copy(f32[1,24,512]{2,1,0:T(8,128)S(1)} %copy-done) | data formatting | bytes 98304
Async XLA Ops:
  26.0 1.4 %copy-start = (f32[1,24,512]{2,1,0:T(8,128)S(1)}, f32[1,24,512]{2,1,0:T(8,128)}, u32[]{:S(2)}) copy-start(f32[1,24,512]{2,1,0:T(8,128)} %get-tuple-element.5) | copy-start | bytes 147460
